TPU v7x, 32 devices: a whole 2x2x4 slice. The times are simulated.
32 devices in a mesh: cells: 8 (over z, x), genes: 4 (over y, core).
Axes of the slice: x: 2, y: 2, z: 4, core: 2. Of those that a mesh axis runs over, the one named last changes fastest.
Arguments:
- counts: int32 [38912, 4000], P('cells', 'genes'), may hold values from 0 to 674, as said below
- sketch: bfloat16 [4000, 128], P('genes'), may hold values from -6 to 6
Outputs:
- basis: float32 [38912, 128], P('cells')
- loadings: float32 [4000, 128], P('genes')
Inputs may be any that keep to these rules, and one draw needn't show every extreme that they name: `counts`: every cell and every gene has a positive total.
All inputs are finite; a program needn't handle non-finite values.
Results may differ from a plain program's by a relative error of at most 0.0051.
Values may be sent and summed in bfloat16 or wider, within the bound.
A program may use at most 128 MiB of HBM per device.

v0:
```python
import math
import jax
import jax.numpy as jnp
from jax import lax
from jax.sharding import PartitionSpec as P

ITERS = 2


def residual_block(block, cell_total, frac, limit):
    values = block.astype(jnp.float32)
    expected = cell_total[:, None] * frac[None, :]
    scaled = (values - expected) / jnp.sqrt(expected + 0.01 * expected * expected)
    return jnp.clip(scaled, -limit, limit).astype(jnp.bfloat16)


def self_gram(block):
    return lax.dot_general(
        block,
        block,
        (((0,), (0,)), ((), ())),
        precision=lax.Precision.HIGHEST,
        preferred_element_type=jnp.float32,
    )


def whitening(gram, count):
    width = gram.shape[0]
    identity = jnp.eye(width, dtype=jnp.float32)
    shifted = gram + 1e-05 * jnp.trace(gram) / width * identity
    lower = jnp.linalg.cholesky(shifted)
    inverse = jax.scipy.linalg.solve_triangular(lower, identity, lower=True)
    return jnp.transpose(inverse) * math.sqrt(count)


def transposed_product(left, right):
    return lax.dot_general(
        left, right, (((0,), (0,)), ((), ())), preferred_element_type=jnp.float32
    )


def loading_total(partial_sum, gene_scale):
    return lax.psum(partial_sum, "cells") * gene_scale


def shards(counts, sketch):
    cell_dev, gene_dev = counts.shape
    group_count = lax.axis_size("genes")
    cell_count = float(cell_dev * lax.axis_size("cells"))
    gene_count = float(gene_dev * group_count)
    cell_part = jnp.sum(counts, axis=1).astype(jnp.float32)
    gene_part = jnp.sum(counts, axis=0).astype(jnp.float32)
    gene_total, group_sum = lax.psum((gene_part, jnp.sum(gene_part)), "cells")
    cell_total, grand = lax.psum((cell_part, group_sum), "genes")
    frac = gene_total / grand
    limit = math.sqrt(cell_count)
    resid = residual_block(counts, cell_total, frac, limit)
    gene_scale = math.sqrt(gene_count) / cell_count
    omega = sketch
    basis = None
    loadings = None
    for sweep in range(ITERS):
        sketched = lax.psum(jnp.dot(resid, omega, preferred_element_type=jnp.float32), "genes")
        gram = lax.psum(self_gram(sketched), "cells")
        basis = jnp.dot(sketched, whitening(gram, cell_count), precision=lax.Precision.HIGHEST)
        partial_sum = transposed_product(resid, basis.astype(jnp.bfloat16))
        loadings = loading_total(partial_sum, gene_scale)
        if sweep < ITERS - 1:
            omega = loadings.astype(jnp.bfloat16)
    return (basis, loadings)


def solution(mesh):
    return jax.shard_map(
        shards,
        mesh=mesh,
        in_specs=(P("cells", "genes"), P("genes", None)),
        out_specs=(P("cells", None), P("genes", None)),
        check_vma=False,
    )
```

profile of v0, /device:TPU:0, one launch (start us, length us, event | category | flops | bytes accessed | tf_op | source)
XLA Modules:
  0.0 572.5 jit_solution(13577707791182518231)
XLA Ops:
  7.2 0.0 all-reduce.9.cloned.1.call-start
  7.2 8.2 %fusion.17 = (s32[4864]{0:T(1024)S(1)}, s32[1000]{0:T(1024)S(1)}) fusion(s32[4864,1000]{0,1:T(8,128)} %param.5), kind=kLoop, calls=%fused_computation.43 | loop fusion | flops 9722136 | bytes 19479456 | tf_op jit(solution)/shard_map/reduce_sum | solution.py:51
  15.4 0.6 convert_reduce_fusion
  16.0 24.0 %all-reduce = (f32[1000]{0:T(1024)S(1)}, f32[]{:T(128)}) all-reduce(f32[1000]{0:T(1024)S(1)} %convert_element_type.29, f32[]{:T(128)} %convert_reduce_fusion), channel_id=1, replica_groups=mesh['cells'=8,'genes'=4] {'cells'}, use_global_device_ids=true, to_apply=%region_3.0 | all-reduce | flops 1001 | bytes 8008 | tf_op jit(solution)/shard_map/psum | solution.py:53
  40.0 11.3 %all-reduce.1 = (f32[]{:T(128)}, f32[4864]{0:T(1024)S(1)}) all-reduce(f32[]{:T(128)} %get-tuple-element.7, f32[4864]{0:T(1024)S(1)} %convert_element_type.28), channel_id=1, replica_groups=mesh['cells'=8,'genes'=4] {'genes'}, use_global_device_ids=true, to_apply=%region_6.0 | all-reduce | flops 4865 | bytes 38920 | tf_op jit(solution)/shard_map/psum | solution.py:54
  51.3 0.6 broadcast_divide_fusion
  51.9 10.2 %fusion.2 = bf16[4864,1000]{0,1:T(8,128)(2,1)S(1)} fusion(s32[4864,1000]{0,1:T(8,128)} %param.5, f32[1000]{0:T(1024)S(1)} %broadcast_divide_fusion, f32[4864]{0:T(1024)S(1)} %get-tuple-element.9), kind=kLoop, calls=%fused_computation.6 | loop fusion | flops 43776000 | bytes 29207456 | tf_op jit(solution)/shard_map/convert_element_type | solution.py:14
  62.1 3.7 copy-done.1
  65.9 4.5 fusion.18
  70.3 0.0 all-reduce.9.cloned.1.call-update
  70.4 0.0 all-reduce.11.cloned.1.call-start
  70.4 54.2 %all-reduce.9.cloned.1.call-done = f32[4864,128]{1,0:T(8,128)} async-done(((f32[4864,128]{1,0:T(8,128)}), f32[4864,128]{1,0:T(8,128)}) %all-reduce.9.cloned.1.call-update) | async-done | bytes 2490384 | tf_op jit(solution)/shard_map/psum | solution.py:63
  124.6 7.3 %fusion.19 = f32[128,128]{0,1:T(8,128)} fusion(f32[4864,128]{1,0:T(8,128)} %all-reduce.9.cloned.1.call-done), kind=kOutput, calls=%fused_computation.45 | convolution fusion | flops 956301312 | bytes 2555904 | tf_op jit(solution)/shard_map/dot_general | solution.py:18
  131.9 0.5 all-reduce.13.cloned.1.call-start
  132.4 69.0 %all-reduce.11.cloned.1.call-done = f32[128,128]{0,1:T(8,128)} async-done(((f32[128,128]{0,1:T(8,128)}), f32[128,128]{0,1:T(8,128)}) %all-reduce.11.cloned.1.call-update) | async-done | bytes 65552 | tf_op jit(solution)/shard_map/psum | solution.py:64
  201.4 1.5 select_reduce_fusion.3
  203.5 0.9 select_add_fusion.1
  204.4 0.1 copy.5
  204.5 0.9 fusion.15
  205.3 11.7 %cholesky.44 = f32[128,128]{1,0:T(8,128)S(1)} custom-call(f32[128,128]{1,0:T(8,128)S(1)} %fusion.15), custom_call_target="Cholesky" | custom-call | tf_op jit(solution)/shard_map/jit(cholesky)/cholesky | solution.py:31
  217.1 0.6 compare_reduce_fusion.1
  217.7 0.7 fusion.10
  218.4 9.8 %custom-call.6 = f32[1,128,128]{1,2,0:T(8,128)S(1)} custom-call(f32[1,128,128]{2,1,0:T(8,128)S(1)} %fusion.10), custom_call_target="InvertDiagBlocksLowerTriangular" | custom-call | tf_op jit(solution)/shard_map/jit(_solve_triangular)/triangular_solve | solution.py:32
  228.2 0.3 convolution_multiply_fusion.1
  228.5 2.1 convolution_convert_fusion
  230.6 7.3 %fusion.20 = f32[1000,128]{1,0:T(8,128)} fusion(bf16[4864,1000]{0,1:T(8,128)(2,1)} %copy-done.1, bf16[4864,128]{1,0:T(8,128)(2,1)S(1)} %convolution_convert_fusion), kind=kOutput, calls=%fused_computation.46 | convolution fusion | flops 1245184000 | bytes 11485184 | tf_op jit(solution)/shard_map/dot_general | solution.py:37
  237.9 0.2 all-reduce.15.cloned.1.call-start
  238.2 72.4 %all-reduce.13.cloned.1.call-done = f32[1000,128]{1,0:T(8,128)} async-done(((f32[1000,128]{1,0:T(8,128)}), f32[1000,128]{1,0:T(8,128)}) %all-reduce.13.cloned.1.call-update) | async-done | bytes 512016 | tf_op jit(solution)/shard_map/psum | solution.py:43
  310.6 8.1 %fusion.6 = f32[4864,128]{1,0:T(8,128)} fusion(bf16[4864,1000]{0,1:T(8,128)(2,1)} %copy-done.1, f32[1000,128]{1,0:T(8,128)} %all-reduce.13.cloned.1.call-done), kind=kOutput, calls=%fused_computation.14 | convolution fusion | flops 1245440000 | bytes 12730368 | tf_op jit(solution)/shard_map/dot_general | solution.py:63
  318.7 0.0 all-reduce.17.cloned.1.call-start
  318.8 57.2 %all-reduce.15.cloned.1.call-done = f32[4864,128]{1,0:T(8,128)} async-done(((f32[4864,128]{1,0:T(8,128)}), f32[4864,128]{1,0:T(8,128)}) %all-reduce.15.cloned.1.call-update) | async-done | bytes 2490384 | tf_op jit(solution)/shard_map/psum | solution.py:63
  375.9 7.3 %fusion.21 = f32[128,128]{0,1:T(8,128)} fusion(f32[4864,128]{1,0:T(8,128)} %all-reduce.15.cloned.1.call-done), kind=kOutput, calls=%fused_computation.47 | convolution fusion | flops 956301312 | bytes 2555904 | tf_op jit(solution)/shard_map/dot_general | solution.py:18
  383.3 0.3 all-reduce.19.cloned.1.call-start
  383.5 69.2 %all-reduce.17.cloned.1.call-done = f32[128,128]{0,1:T(8,128)} async-done(((f32[128,128]{0,1:T(8,128)}), f32[128,128]{0,1:T(8,128)}) %all-reduce.17.cloned.1.call-update) | async-done | bytes 65552 | tf_op jit(solution)/shard_map/psum | solution.py:64
  452.8 1.5 select_reduce_fusion.2
  454.9 0.9 select_add_fusion
  455.7 0.1 copy.7
  455.8 0.9 fusion.13
  456.7 11.7 %cholesky.55 = f32[128,128]{1,0:T(8,128)S(1)} custom-call(f32[128,128]{1,0:T(8,128)S(1)} %fusion.13), custom_call_target="Cholesky" | custom-call | tf_op jit(solution)/shard_map/jit(cholesky)/cholesky | solution.py:31
  468.5 0.6 compare_reduce_fusion
  469.1 0.7 fusion.11
  469.8 9.8 %custom-call.7 = f32[1,128,128]{1,2,0:T(8,128)S(1)} custom-call(f32[1,128,128]{2,1,0:T(8,128)S(1)} %fusion.11), custom_call_target="InvertDiagBlocksLowerTriangular" | custom-call | tf_op jit(solution)/shard_map/jit(_solve_triangular)/triangular_solve | solution.py:32
  479.6 0.3 convolution_multiply_fusion
  479.9 2.2 fusion.22
  482.1 1.4 copy-done.4
  483.5 7.3 %fusion.4 = f32[1000,128]{1,0:T(8,128)} fusion(bf16[4864,1000]{0,1:T(8,128)(2,1)} %copy-done.1, f32[4864,128]{1,0:T(8,128)S(1)} %fusion.22), kind=kOutput, calls=%fused_computation.9 | convolution fusion | flops 1245806592 | bytes 12730368 | tf_op jit(solution)/shard_map/dot_general | solution.py:37
  490.8 72.7 %all-reduce.19.cloned.1.call-done = f32[1000,128]{1,0:T(8,128)} async-done(((f32[1000,128]{1,0:T(8,128)}), f32[1000,128]{1,0:T(8,128)}) %all-reduce.19.cloned.1.call-update) | async-done | bytes 512016 | tf_op jit(solution)/shard_map/psum | solution.py:43
  563.5 1.9 broadcast_multiply_fusion
  (17 shorter events, 0.2 us)
Async XLA Ops:
  7.2 58.7 %copy-start = (bf16[1000,128]{1,0:T(8,128)(2,1)S(1)}, bf16[1000,128]{1,0:T(8,128)(2,1)}, u32[]{:S(2)}) copy-start(bf16[1000,128]{1,0:T(8,128)(2,1)} %param.6) | copy-start | bytes 768004
  7.2 117.4 %all-reduce.9.cloned.1.call-start = ((), (), s32[]{:S(2)}) async-start(), calls=%async_computation | async-start | bytes 4980736 | tf_op jit(solution)/shard_map/psum | solution.py:63
  62.1 3.7 copy-start.1
  70.4 131.0 %all-reduce.11.cloned.1.call-start = ((), (), s32[]{:S(2)}) async-start(), calls=%async_computation.1 | async-start | bytes 131072 | tf_op jit(solution)/shard_map/psum | solution.py:64
  124.6 103.9 %copy-start.3 = (f32[4864,128]{1,0:T(8,128)S(1)}, f32[4864,128]{1,0:T(8,128)}, u32[]{:S(2)}) copy-start(f32[4864,128]{1,0:T(8,128)} %all-reduce.9.cloned.1.call-done) | copy-start | bytes 7471108
  131.9 178.7 %all-reduce.13.cloned.1.call-start = ((), (), s32[]{:S(2)}) async-start(), calls=%async_computation.2 | async-start | bytes 1024000 | tf_op jit(solution)/shard_map/psum | solution.py:43
  237.9 138.0 %all-reduce.15.cloned.1.call-start = ((), (), s32[]{:S(2)}) async-start(), calls=%async_computation.3 | async-start | bytes 4980736 | tf_op jit(solution)/shard_map/psum | solution.py:63
  318.7 134.0 %all-reduce.17.cloned.1.call-start = ((), (), s32[]{:S(2)}) async-start(), calls=%async_computation.4 | async-start | bytes 131072 | tf_op jit(solution)/shard_map/psum | solution.py:64
  375.9 103.9 %copy-start.2 = (f32[4864,128]{1,0:T(8,128)S(1)}, f32[4864,128]{1,0:T(8,128)}, u32[]{:S(2)}) copy-start(f32[4864,128]{1,0:T(8,128)} %all-reduce.15.cloned.1.call-done) | copy-start | bytes 7471108
  383.3 180.2 %all-reduce.19.cloned.1.call-start = ((), (), s32[]{:S(2)}) async-start(), calls=%async_computation.5 | async-start | bytes 1024000 | tf_op jit(solution)/shard_map/psum | solution.py:43
  482.1 1.5 copy-start.4
Sparse Core Ops, SparseCore 0:
  70.5 54.0 all-reduce.8
  132.0 69.3 all-reduce.10
  238.0 72.4 all-reduce.12
  318.9 57.0 all-reduce.14
  383.4 69.3 all-reduce.16
  491.0 72.5 all-reduce.18
where the time goes:
time: 581 us; the launch traced here: 572 us
  waiting for transfers between devices  395 us (68%)
  other arithmetic  73.6 us (13%)
  matrix products  46.6 us (8%)
  blocking collectives  35.3 us (6%)
  between operations  15.8 us (3%)
    psum x2, waiting for transfers between devices, loading_total(): return lax.psum(partial_sum, 'cells') * gene_scale  145 us
    psum x2, waiting for transfers between devices, shards(): gram = lax.psum(self_gram(sketched), 'cells')  138 us
    psum x2, waiting for transfers between devices, shards(): lax.psum(jnp.dot(resid, omega, preferred_element_type=jnp.float32), 'genes')  111 us
    another operation x6, other arithmetic, whitening(): lower = jnp.linalg.cholesky(shifted)  24.8 us
    psum x1, blocking collectives, shards(): gene_total, group_sum = lax.psum((gene_part, jnp.sum(gene_part)), 'cells')  24 us
    another operation x4, other arithmetic, whitening(): inverse = jax.scipy.linalg.solve_triangular(lower, identity, lower=True)  20.9 us
    dot_general x2, matrix products, self_gram(): lax.dot_general(block, block, (((0,), (0,)), ((), ())), precision=lax.Pre...  14.6 us
    dot_general x2, matrix products, transposed_product(): lax.dot_general(left, right, (((0,), (0,)), ((), ())), preferred_element_...  14.6 us
  transfers between devices with their start and end apart: 6, of which 6 were waited for; matrix products, arithmetic and copies ran while one was open for 0% of the time, Pallas kernels for 0%

commit v1 on v0

--- a/solution.py
+++ b/solution.py
@@ -61,7 +61,7 @@
     loadings = None
     for sweep in range(ITERS):
         sketched = lax.psum(jnp.dot(resid, omega, preferred_element_type=jnp.float32), "genes")
-        gram = lax.psum(self_gram(sketched), "cells")
+        gram = jnp.sum(lax.all_gather(self_gram(sketched), "cells"), axis=0)
         basis = jnp.dot(sketched, whitening(gram, cell_count), precision=lax.Precision.HIGHEST)
         partial_sum = transposed_product(resid, basis.astype(jnp.bfloat16))
         loadings = loading_total(partial_sum, gene_scale)

time: 581 us -> 499 us (0.86)
  waiting for transfers between devices: 395 us -> 256 us
  blocking collectives: 35.3 us -> 99.3 us
    psum x2 -> x0, waiting for transfers between devices: 138 us -> none  [shards(): gram = lax.psum(self_gram(sketched), 'cells')]
    all_gather x0 -> x2, blocking collectives: none -> 64 us  [shards(): gram = jnp.sum(lax.all_gather(self_gram(sketched), 'cells'), axis=0)]
  transfers between devices with their start and end apart: 6 -> 4, of which waited for: 6 -> 4; matrix products, arithmetic and copies ran while one was open for 0% -> 0% of each run, Pallas kernels for 0% -> 0%
where the time goes in v1:
time: 499 us; the launch traced here: 491 us
  waiting for transfers between devices  256 us (51%)
  blocking collectives  99.3 us (20%)
  other arithmetic  68.6 us (14%)
  matrix products  45.3 us (9%)
  between operations  15.5 us (3%)
  local copies, waits for them, and re-layouts  5.54 us (1%)
    psum x2, waiting for transfers between devices, loading_total(): return lax.psum(partial_sum, 'cells') * gene_scale  145 us
    psum x2, waiting for transfers between devices, shards(): lax.psum(jnp.dot(resid, omega, preferred_element_type=jnp.float32), 'genes')  111 us
    all_gather x2, blocking collectives, shards(): gram = jnp.sum(lax.all_gather(self_gram(sketched), 'cells'), axis=0)  64 us
    another operation x6, other arithmetic, whitening(): lower = jnp.linalg.cholesky(shifted)  24.8 us
    psum x1, blocking collectives, shards(): gene_total, group_sum = lax.psum((gene_part, jnp.sum(gene_part)), 'cells')  24 us
    another operation x4, other arithmetic, whitening(): inverse = jax.scipy.linalg.solve_triangular(lower, identity, lower=True)  20.9 us
    dot_general x2, matrix products, transposed_product(): lax.dot_general(left, right, (((0,), (0,)), ((), ())), preferred_element_...  14.6 us
    dot_general x2, matrix products, self_gram(): lax.dot_general(block, block, (((0,), (0,)), ((), ())), precision=lax.Pre...  13.3 us
  transfers between devices with their start and end apart: 4, of which 4 were waited for; matrix products, arithmetic and copies ran while one was open for 0% of the time, Pallas kernels for 0%

profile of v1, /device:TPU:0, one launch (start us, length us, event | category | flops | bytes accessed | tf_op | source)
XLA Modules:
  0.0 491.0 jit_solution(16428461358649345848)
XLA Ops:
  7.2 0.0 copy-start
  7.2 0.0 all-reduce.7.cloned.1.call-start
  7.2 8.2 %fusion.17 = (s32[4864]{0:T(1024)S(1)}, s32[1000]{0:T(1024)S(1)}) fusion(s32[4864,1000]{0,1:T(8,128)} %param.5), kind=kLoop, calls=%fused_computation.43 | loop fusion | flops 9722136 | bytes 19479456 | tf_op jit(solution)/shard_map/reduce_sum | solution.py:51
  15.4 0.6 convert_reduce_fusion
  16.0 24.0 %all-reduce = (f32[1000]{0:T(1024)S(1)}, f32[]{:T(128)}) all-reduce(f32[1000]{0:T(1024)S(1)} %convert_element_type.29, f32[]{:T(128)} %convert_reduce_fusion), channel_id=1, replica_groups=mesh['cells'=8,'genes'=4] {'cells'}, use_global_device_ids=true, to_apply=%region_3.0 | all-reduce | flops 1001 | bytes 8008 | tf_op jit(solution)/shard_map/psum | solution.py:53
  40.0 11.3 %all-reduce.1 = (f32[]{:T(128)}, f32[4864]{0:T(1024)S(1)}) all-reduce(f32[]{:T(128)} %get-tuple-element.7, f32[4864]{0:T(1024)S(1)} %convert_element_type.28), channel_id=1, replica_groups=mesh['cells'=8,'genes'=4] {'genes'}, use_global_device_ids=true, to_apply=%region_6.0 | all-reduce | flops 4865 | bytes 38920 | tf_op jit(solution)/shard_map/psum | solution.py:54
  51.3 0.6 broadcast_divide_fusion
  51.9 10.2 %fusion.2 = bf16[4864,1000]{0,1:T(8,128)(2,1)S(1)} fusion(s32[4864,1000]{0,1:T(8,128)} %param.5, f32[1000]{0:T(1024)S(1)} %broadcast_divide_fusion, f32[4864]{0:T(1024)S(1)} %get-tuple-element.9), kind=kLoop, calls=%fused_computation.6 | loop fusion | flops 43776000 | bytes 29207456 | tf_op jit(solution)/shard_map/convert_element_type | solution.py:14
  62.1 3.7 copy-done.1
  65.9 4.5 fusion.18
  70.3 0.0 all-reduce.7.cloned.1.call-update
  70.4 0.0 all-reduce.9.cloned.1.call-start
  70.4 54.2 %all-reduce.7.cloned.1.call-done = f32[4864,128]{1,0:T(8,128)} async-done(((f32[4864,128]{1,0:T(8,128)}), f32[4864,128]{1,0:T(8,128)}) %all-reduce.7.cloned.1.call-update) | async-done | bytes 2490384 | tf_op jit(solution)/shard_map/psum | solution.py:63
  124.6 6.7 %fusion.19 = f32[128,128]{1,0:T(8,128)S(1)} fusion(f32[4864,128]{1,0:T(8,128)} %all-reduce.7.cloned.1.call-done), kind=kOutput, calls=%fused_computation.45 | convolution fusion | flops 956301312 | bytes 2555904 | tf_op jit(solution)/shard_map/dot_general | solution.py:18
  131.2 32.1 %all-gather = f32[1024,128]{1,0:T(8,128)S(1)} all-gather(f32[128,128]{1,0:T(8,128)S(1)} %fusion.19), channel_id=2, replica_groups=mesh['cells'=8,'genes'=4] {'cells'}, dimensions={0}, use_global_device_ids=true | all-gather | bytes 589824 | tf_op jit(solution)/shard_map/all_gather | solution.py:64
  163.4 0.1 copy.7
  163.5 0.6 select_reduce_fusion.3
  164.8 0.1 copy.8
  164.9 11.7 %cholesky.44 = f32[128,128]{1,0:T(8,128)S(1)} custom-call(f32[128,128]{1,0:T(8,128)S(1)} %fusion.15), custom_call_target="Cholesky" | custom-call | tf_op jit(solution)/shard_map/jit(cholesky)/cholesky | solution.py:31
  176.7 0.6 compare_reduce_fusion.1
  177.3 0.7 fusion.10
  178.0 9.8 %custom-call.6 = f32[1,128,128]{1,2,0:T(8,128)S(1)} custom-call(f32[1,128,128]{2,1,0:T(8,128)S(1)} %fusion.10), custom_call_target="InvertDiagBlocksLowerTriangular" | custom-call | tf_op jit(solution)/shard_map/jit(_solve_triangular)/triangular_solve | solution.py:32
  187.8 0.3 convolution_multiply_fusion.1
  188.1 2.1 convolution_convert_fusion
  190.2 7.3 %fusion.20 = f32[1000,128]{1,0:T(8,128)} fusion(bf16[4864,1000]{0,1:T(8,128)(2,1)} %copy-done.1, bf16[4864,128]{1,0:T(8,128)(2,1)S(1)} %convolution_convert_fusion), kind=kOutput, calls=%fused_computation.46 | convolution fusion | flops 1245184000 | bytes 11485184 | tf_op jit(solution)/shard_map/dot_general | solution.py:37
  197.5 0.0 all-reduce.9.cloned.1.call-update
  197.5 0.2 all-reduce.11.cloned.1.call-start
  197.7 72.4 %all-reduce.9.cloned.1.call-done = f32[1000,128]{1,0:T(8,128)} async-done(((f32[1000,128]{1,0:T(8,128)}), f32[1000,128]{1,0:T(8,128)}) %all-reduce.9.cloned.1.call-update) | async-done | bytes 512016 | tf_op jit(solution)/shard_map/psum | solution.py:43
  270.1 8.1 %fusion.6 = f32[4864,128]{1,0:T(8,128)} fusion(bf16[4864,1000]{0,1:T(8,128)(2,1)} %copy-done.1, f32[1000,128]{1,0:T(8,128)} %all-reduce.9.cloned.1.call-done), kind=kOutput, calls=%fused_computation.14 | convolution fusion | flops 1245440000 | bytes 12730368 | tf_op jit(solution)/shard_map/dot_general | solution.py:63
  278.3 0.0 all-reduce.11.cloned.1.call-update
  278.3 0.0 all-reduce.13.cloned.1.call-start
  278.3 57.2 %all-reduce.11.cloned.1.call-done = f32[4864,128]{1,0:T(8,128)} async-done(((f32[4864,128]{1,0:T(8,128)}), f32[4864,128]{1,0:T(8,128)}) %all-reduce.11.cloned.1.call-update) | async-done | bytes 2490384 | tf_op jit(solution)/shard_map/psum | solution.py:63
  335.5 6.7 %fusion.21 = f32[128,128]{1,0:T(8,128)S(1)} fusion(f32[4864,128]{1,0:T(8,128)} %all-reduce.11.cloned.1.call-done), kind=kOutput, calls=%fused_computation.47 | convolution fusion | flops 956301312 | bytes 2555904 | tf_op jit(solution)/shard_map/dot_general | solution.py:18
  342.2 31.9 %all-gather.1 = f32[1024,128]{1,0:T(8,128)S(1)} all-gather(f32[128,128]{1,0:T(8,128)S(1)} %fusion.21), channel_id=3, replica_groups=mesh['cells'=8,'genes'=4] {'cells'}, dimensions={0}, use_global_device_ids=true | all-gather | bytes 589824 | tf_op jit(solution)/shard_map/all_gather | solution.py:64
  374.1 0.1 copy.10
  374.2 0.6 select_reduce_fusion.2
  375.5 0.1 copy.11
  375.6 11.7 %cholesky.55 = f32[128,128]{1,0:T(8,128)S(1)} custom-call(f32[128,128]{1,0:T(8,128)S(1)} %fusion.13), custom_call_target="Cholesky" | custom-call | tf_op jit(solution)/shard_map/jit(cholesky)/cholesky | solution.py:31
  387.3 0.6 compare_reduce_fusion
  388.0 0.7 fusion.11
  388.6 9.8 %custom-call.7 = f32[1,128,128]{1,2,0:T(8,128)S(1)} custom-call(f32[1,128,128]{2,1,0:T(8,128)S(1)} %fusion.11), custom_call_target="InvertDiagBlocksLowerTriangular" | custom-call | tf_op jit(solution)/shard_map/jit(_solve_triangular)/triangular_solve | solution.py:32
  398.5 0.3 convolution_multiply_fusion
  398.8 2.2 fusion.22
  401.0 1.4 copy-done.4
  402.4 7.3 %fusion.4 = f32[1000,128]{1,0:T(8,128)} fusion(bf16[4864,1000]{0,1:T(8,128)(2,1)} %copy-done.1, f32[4864,128]{1,0:T(8,128)S(1)} %fusion.22), kind=kOutput, calls=%fused_computation.9 | convolution fusion | flops 1245806592 | bytes 12730368 | tf_op jit(solution)/shard_map/dot_general | solution.py:37
  409.7 0.0 all-reduce.13.cloned.1.call-update
  409.7 72.7 %all-reduce.13.cloned.1.call-done = f32[1000,128]{1,0:T(8,128)} async-done(((f32[1000,128]{1,0:T(8,128)}), f32[1000,128]{1,0:T(8,128)}) %all-reduce.13.cloned.1.call-update) | async-done | bytes 512016 | tf_op jit(solution)/shard_map/psum | solution.py:43
  482.4 1.9 broadcast_multiply_fusion
  (17 shorter events, 0.2 us)
Async XLA Ops:
  7.2 58.7 %copy-start = (bf16[1000,128]{1,0:T(8,128)(2,1)S(1)}, bf16[1000,128]{1,0:T(8,128)(2,1)}, u32[]{:S(2)}) copy-start(bf16[1000,128]{1,0:T(8,128)(2,1)} %param.6) | copy-start | bytes 768004
  7.2 117.4 %all-reduce.7.cloned.1.call-start = ((), (), s32[]{:S(2)}) async-start(), calls=%async_computation | async-start | bytes 4980736 | tf_op jit(solution)/shard_map/psum | solution.py:63
  62.1 3.7 copy-start.1
  70.4 199.8 %all-reduce.9.cloned.1.call-start = ((), (), s32[]{:S(2)}) async-start(), calls=%async_computation.1 | async-start | bytes 1024000 | tf_op jit(solution)/shard_map/psum | solution.py:43
  124.6 63.5 %copy-start.3 = (f32[4864,128]{1,0:T(8,128)S(1)}, f32[4864,128]{1,0:T(8,128)}, u32[]{:S(2)}) copy-start(f32[4864,128]{1,0:T(8,128)} %all-reduce.7.cloned.1.call-done) | copy-start | bytes 7471108
  197.5 138.0 %all-reduce.11.cloned.1.call-start = ((), (), s32[]{:S(2)}) async-start(), calls=%async_computation.2 | async-start | bytes 4980736 | tf_op jit(solution)/shard_map/psum | solution.py:63
  278.3 204.1 %all-reduce.13.cloned.1.call-start = ((), (), s32[]{:S(2)}) async-start(), calls=%async_computation.3 | async-start | bytes 1024000 | tf_op jit(solution)/shard_map/psum | solution.py:43
  335.5 63.3 %copy-start.2 = (f32[4864,128]{1,0:T(8,128)S(1)}, f32[4864,128]{1,0:T(8,128)}, u32[]{:S(2)}) copy-start(f32[4864,128]{1,0:T(8,128)} %all-reduce.11.cloned.1.call-done) | copy-start | bytes 7471108
  400.9 1.5 copy-start.4
Sparse Core Ops, SparseCore 0:
  70.5 54.0 all-reduce.6
  197.6 72.4 all-reduce.8
  278.4 57.0 all-reduce.10
  409.8 72.5 all-reduce.12
